TPU v7x, 32 devices: a whole 2x2x4 slice. The times are simulated.
32 devices in a mesh: cz: 4 (over z), cy: 2 (over y), cx: 4 (over x, core).
Axes of the slice: x: 2, y: 2, z: 4, core: 2. Of those that a mesh axis runs over, the one named last changes fastest.
Arguments:
- x: bfloat16 [1024, 4096], P(('cx', 'cz'), 'cy')
- w1: bfloat16 [4096, 16384], P('cy', ('cz', 'cx'))
- w2: bfloat16 [16384, 4096], P('cz', ('cy', 'cx'))
Outputs:
- output: bfloat16 [1024, 4096], P(('cx', 'cz'), 'cy')
All inputs are finite; a program needn't handle non-finite values.
Results may differ from a plain program's by a relative error of at most 0.0115307.
Values are sent between devices in bfloat16 or wider.
A program may use at most 1 GiB of HBM per device.

v0:
```python
import jax
import jax.numpy as jnp
from jax import lax
from jax.sharding import PartitionSpec as P


def solution(mesh):
    def body(x, w1, w2):
        xg = lax.all_gather(x, "cz", axis=0, tiled=True)
        w1g = lax.all_gather(w1, "cx", axis=1, tiled=True)
        cp = jnp.dot(xg, w1g, preferred_element_type=jnp.float32)
        c = lax.psum_scatter(cp, "cy", scatter_dimension=0, tiled=True).astype(jnp.bfloat16)
        h = jax.nn.gelu(c.astype(jnp.float32), approximate=True).astype(jnp.bfloat16)
        hg = lax.all_gather(h, "cy", axis=0, tiled=True)
        w2g = lax.all_gather(w2, "cx", axis=1, tiled=True)
        zp = jnp.dot(hg, w2g, preferred_element_type=jnp.float32)
        return lax.psum_scatter(zp, "cz", scatter_dimension=0, tiled=True).astype(jnp.bfloat16)

    return jax.shard_map(
        body,
        mesh=mesh,
        in_specs=(P(("cx", "cz"), "cy"), P("cy", ("cz", "cx")), P("cz", ("cy", "cx"))),
        out_specs=P(("cx", "cz"), "cy"),
        check_vma=False,
    )
```

profile of v0, /device:TPU:0, one launch (start us, length us, event | category | flops | bytes accessed | tf_op | source)
XLA Modules:
  0.0 422.2 jit_solution(11122629416097555318)
XLA Ops:
  6.5 0.0 all-gather.5.cloned.1.call-start
  6.5 0.7 all-gather.5.cloned.1.call-update
  7.3 0.0 all-gather.7.cloned.1.call-start
  7.3 0.7 all-gather.7.cloned.1.call-update
  8.0 0.0 reduce-scatter.3.cloned.1.call-start
  8.1 31.5 %all-gather.5.cloned.1.call-done = bf16[256,2048]{1,0:T(8,128)(2,1)} async-done(((bf16[64,2048]{1,0:T(8,128)(2,1)}), bf16[256,2048]{1,0:T(8,128)(2,1)}) %all-gather.5.cloned.1.call-update) | async-done | bytes 1048592 | tf_op jit(solution)/shard_map/all_gather | solution.py:9
  39.6 107.9 %all-gather.7.cloned.1.call-done = bf16[2048,4096]{1,0:T(8,128)(2,1)} async-done(((bf16[2048,1024]{1,0:T(8,128)(2,1)}), bf16[2048,4096]{1,0:T(8,128)(2,1)}) %all-gather.7.cloned.1.call-update) | async-done | bytes 16777232 | tf_op jit(solution)/shard_map/all_gather | solution.py:10
  147.5 12.5 %fusion.6 = f32[256,4096]{1,0:T(8,128)} fusion(bf16[256,2048]{1,0:T(8,128)(2,1)} %all-gather.5.cloned.1.call-done, bf16[2048,4096]{1,0:T(8,128)(2,1)} %all-gather.7.cloned.1.call-done), kind=kOutput, calls=%fused_computation.10 | convolution fusion | flops 4294967296 | bytes 22020096 | tf_op jit(solution)/shard_map/dot_general | solution.py:11
  160.1 0.0 reduce-scatter.3.cloned.1.call-update
  160.1 0.0 all-gather.11.cloned.1.call-start
  160.1 0.5 all-gather.11.cloned.1.call-update
  160.7 0.0 all-gather.9.cloned.1.call-start
  160.7 53.8 %reduce-scatter.3.cloned.1.call-done = f32[128,4096]{1,0:T(8,128)} async-done(((f32[256,4096]{1,0:T(8,128)}), f32[128,4096]{1,0:T(8,128)}) %reduce-scatter.3.cloned.1.call-update) | async-done | bytes 2097168 | tf_op jit(solution)/shard_map/reduce_scatter | solution.py:12
  214.5 3.2 fusion.5
  217.7 0.0 all-gather.9.cloned.1.call-update
  217.8 0.0 reduce-scatter.5.cloned.1.call-start
  217.8 105.1 %all-gather.11.cloned.1.call-done = bf16[4096,2048]{1,0:T(8,128)(2,1)} async-done(((bf16[4096,512]{1,0:T(8,128)(2,1)}), bf16[4096,2048]{1,0:T(8,128)(2,1)}) %all-gather.11.cloned.1.call-update) | async-done | bytes 16777232 | tf_op jit(solution)/shard_map/all_gather | solution.py:15
  322.9 34.3 %all-gather.9.cloned.1.call-done = bf16[256,4096]{1,0:T(8,128)(2,1)} async-done(((bf16[128,4096]{1,0:T(8,128)(2,1)}), bf16[256,4096]{1,0:T(8,128)(2,1)}) %all-gather.9.cloned.1.call-update) | async-done | bytes 2097168 | tf_op jit(solution)/shard_map/all_gather | solution.py:14
  357.3 12.2 %fusion.7 = f32[256,2048]{1,0:T(8,128)} fusion(bf16[256,4096]{1,0:T(8,128)(2,1)} %all-gather.9.cloned.1.call-done, bf16[4096,2048]{1,0:T(8,128)(2,1)} %all-gather.11.cloned.1.call-done), kind=kOutput, calls=%fused_computation.11 | convolution fusion | flops 4294967296 | bytes 20971520 | tf_op jit(solution)/shard_map/dot_general | solution.py:16
  369.5 0.0 reduce-scatter.5.cloned.1.call-update
  369.5 44.1 %reduce-scatter.5.cloned.1.call-done = f32[64,2048]{1,0:T(8,128)} async-done(((f32[256,2048]{1,0:T(8,128)}), f32[64,2048]{1,0:T(8,128)}) %reduce-scatter.5.cloned.1.call-update) | async-done | bytes 524304 | tf_op jit(solution)/shard_map/reduce_scatter | solution.py:17
  413.6 1.8 convert_element_type.15
Async XLA Ops:
  6.5 33.1 %all-gather.5.cloned.1.call-start = ((), (), s32[]{:S(2)}) async-start(), calls=%async_computation.2 | async-start | bytes 1310720 | tf_op jit(solution)/shard_map/all_gather | solution.py:9
  7.3 140.3 %all-gather.7.cloned.1.call-start = ((), (), s32[]{:S(2)}) async-start(), calls=%async_computation.3 | async-start | bytes 20971520 | tf_op jit(solution)/shard_map/all_gather | solution.py:10
  8.0 206.5 %reduce-scatter.3.cloned.1.call-start = ((), (), s32[]{:S(2)}) async-start(), calls=%async_computation.4 | async-start | bytes 6291456 | tf_op jit(solution)/shard_map/reduce_scatter | solution.py:12
  160.1 162.8 %all-gather.11.cloned.1.call-start = ((), (), s32[]{:S(2)}) async-start(), calls=%async_computation.6 | async-start | bytes 20971520 | tf_op jit(solution)/shard_map/all_gather | solution.py:15
  160.7 196.6 %all-gather.9.cloned.1.call-start = ((), (), s32[]{:S(2)}) async-start(), calls=%async_computation.5 | async-start | bytes 3145728 | tf_op jit(solution)/shard_map/all_gather | solution.py:14
  217.8 195.8 %reduce-scatter.5.cloned.1.call-start = ((), (), s32[]{:S(2)}) async-start(), calls=%async_computation.7 | async-start | bytes 2621440 | tf_op jit(solution)/shard_map/reduce_scatter | solution.py:17
Sparse Core Ops, SparseCore 0:
  8.9 30.6 all-gather.4
  41.2 106.3 all-gather.6
  160.2 54.2 reduce-scatter.2
  215.9 106.9 all-gather.10
  324.3 32.9 all-gather.8
  369.6 43.9 reduce-scatter.4
where the time goes:
time: 422 us
  waiting for transfers between devices  379 us (90%)
  matrix products  24.8 us (6%)
  between operations  13.5 us (3%)
  other arithmetic  4.98 us (1%)
    all_gather x1, waiting for transfers between devices, body(): w1g = lax.all_gather(w1, 'cx', axis=1, tiled=True)  108 us
    all_gather x1, waiting for transfers between devices, body(): w2g = lax.all_gather(w2, 'cx', axis=1, tiled=True)  105 us
    reduce_scatter x1, waiting for transfers between devices, body(): lax.psum_scatter(cp, 'cy', scatter_dimension=0, tiled=True)  53.8 us
    reduce_scatter x1, waiting for transfers between devices, body(): lax.psum_scatter(zp, 'cz', scatter_dimension=0, tiled=True)  44.1 us
    all_gather x1, waiting for transfers between devices, body(): hg = lax.all_gather(h, 'cy', axis=0, tiled=True)  34.3 us
    all_gather x1, waiting for transfers between devices, body(): xg = lax.all_gather(x, 'cz', axis=0, tiled=True)  31.5 us
    dot_general x1, matrix products, body(): cp = jnp.dot(xg, w1g, preferred_element_type=jnp.float32)  12.5 us
    dot_general x1, matrix products, body(): zp = jnp.dot(hg, w2g, preferred_element_type=jnp.float32)  12.2 us
  transfers between devices with their start and end apart: 6, of which 6 were waited for; matrix products, arithmetic and copies ran while one was open for 1% of the time, Pallas kernels for 0%

commit v1 on v0

v1 whole, which is shorter than its diff:
```python
import math

import jax
import jax.numpy as jnp
from jax import lax
from jax.experimental import pallas as pl
from jax.experimental.pallas import tpu as pltpu
from jax.sharding import PartitionSpec as P

MESH = pl.DeviceIdType.MESH
ROWS = 64
HALF = ROWS // 2
BLOCKS = 16
LEAD = 2


def kernel(x_hbm, w1_hbm, w2_hbm, out_ref, xg, w1, w2, cp, crv, hg, zp, zu, zd, fb, ab, ld,
           x_xs, x_xr, x_ds, x_dr, x_us, x_ur, x_ns, x_nr, cs, cr, hys, hyr, hxs, hxr, gxs, gxr,
           d0s, d0r, d1s, d1r, zs, zur, znr, a_s, a_r):
    z, y, cx = lax.axis_index("cz"), lax.axis_index("cy"), lax.axis_index("cx")
    core = cx % 2
    xp = (cx + 2) % 4
    sib = cx + 1 - 2 * core
    sibxp = (sib + 2) % 4
    dev_y = (z, 1 - y, cx)
    dev_x = (z, y, xp)
    dev_s = (z, y, sib)
    dev_up = ((z + 1) % 4, y, cx)
    dev_dn = ((z + 3) % 4, y, cx)
    width = w1.shape[1]

    loads = [pltpu.make_async_copy(x_hbm, xg.at[z * 4 + cx], ld.at[0]),
             pltpu.make_async_copy(w1_hbm, w1, ld.at[1]),
             pltpu.make_async_copy(w2_hbm, w2, ld.at[2])]
    for load in loads:
        load.start()

    barrier = pltpu.get_barrier_semaphore()
    for dev in (dev_y, dev_x, dev_s, (z, y, sibxp)):
        pl.semaphore_signal(barrier, inc=1, device_id=dev, device_id_type=MESH)

    @pl.when(z < 3)
    def _():
        pl.semaphore_signal(barrier, inc=1, device_id=dev_up, device_id_type=MESH)

    @pl.when(z > 0)
    def _():
        pl.semaphore_signal(barrier, inc=1, device_id=dev_dn, device_id_type=MESH)

    edge = (z == 0) | (z == 3)

    @pl.when(edge)
    def _():
        pl.semaphore_wait(barrier, 5)

    @pl.when(jnp.logical_not(edge))
    def _():
        pl.semaphore_wait(barrier, 6)

    def rc(src, dst, ssem, rsem, dev):
        return pltpu.make_async_remote_copy(src_ref=src, dst_ref=dst, send_sem=ssem, recv_sem=rsem,
                                            device_id=dev, device_id_type=MESH)

    mine = pl.ds(pl.multiple_of(y * HALF, HALF), HALF)
    other = pl.ds(pl.multiple_of((1 - y) * HALF, HALF), HALF)

    def t_xx(b):
        return rc(xg.at[b], xg.at[b], x_xs, x_xr, dev_x)

    def t_xd(b):
        return rc(xg.at[b], xg.at[b], x_ds.at[b], x_dr.at[b], dev_s)

    def t_xu(b):
        return rc(xg.at[b], xg.at[b], x_us.at[b], x_ur.at[b], dev_up)

    def t_xn(b):
        return rc(xg.at[b], xg.at[b], x_ns.at[b], x_nr.at[b], dev_dn)

    def t_c(b):
        return rc(cp.at[b, other], crv.at[b], cs.at[b], cr.at[b], dev_y)

    def t_hy(b, rows):
        return rc(hg.at[b, cx, rows], hg.at[b, cx, rows], hys.at[b], hyr.at[b], dev_y)

    def t_hx(b, c, rows):
        return rc(hg.at[b, c, rows], hg.at[b, c, rows], hxs.at[b], hxr.at[b], dev_x)

    def t_gx(b, c, rows):
        return rc(hg.at[b, c, rows], hg.at[b, c, rows], gxs.at[b], gxr.at[b], dev_x)

    def t_d0(b, c):
        return rc(hg.at[b, c], hg.at[b, c], d0s.at[b], d0r.at[b], dev_s)

    def t_d1(b, c):
        return rc(hg.at[b, c], hg.at[b, c], d1s.at[b], d1r.at[b], dev_s)

    def t_zu(b):
        return rc(zp.at[b], zu.at[b], zs.at[b], zur.at[b], dev_up)

    def t_zn(b):
        return rc(zp.at[b], zd.at[b], zs.at[b], znr.at[b], dev_dn)

    low = 1 - z // 2

    def plane(s):
        return jnp.where(s == 0, z, jnp.where(s == 1, 1 + low, jnp.where(s == 2, 3 * low, z + 1 - 2 * (z % 2))))

    def xor(a, b):
        return ((a // 2 + b // 2) % 2) * 2 + (a + b) % 2

    def block(n, me):
        s, j = n // 4, n % 4
        return plane(s) * 4 + jnp.where(s < 2, xor(me, j), j)

    def when(cond):
        return pl.when(cond)

    loads[0].wait()
    own = z * 4 + cx
    far = z * 4 + xp
    t_xx(own).start()
    t_xd(own).start()

    @when(z < 3)
    def _():
        t_xu(own).start()

    @when(z > 0)
    def _():
        t_xn(own).start()

    def x_from_partner():
        t_xx(far).wait_recv()
        t_xd(far).start()

        @when(z < 2)
        def _():
            t_xu(far).start()

        @when(z > 1)
        def _():
            t_xn(far).start()

    def x_late():
        @when(z == 2)
        def _():
            t_xu(far).start()

        @when(z == 1)
        def _():
            t_xn(far).start()

    def x_hop(dist, c):
        @when(z >= dist)
        def _():
            b = (z - dist) * 4 + c
            t_xu(b).wait_recv()
            t_xd(b).start()

            @when(z < 3)
            def _():
                t_xu(b).start()

        @when(z + dist < 4)
        def _():
            b = (z + dist) * 4 + c
            t_xn(b).wait_recv()
            t_xd(b).start()

            @when(z > 0)
            def _():
                t_xn(b).start()

    def first_matmul(n):
        b = block(n, cx)

        @when((b + cx) % 2 == 1)
        def _():
            t_xd(b).wait_recv()

        cp[b] = jnp.dot(xg[b], w1[...], preferred_element_type=jnp.float32)
        t_c(b).start()

    def activation(n):
        b = block(n, cx)
        t_c(b).wait_recv()
        c = (cp[b, mine] + crv[b]).astype(jnp.bfloat16).astype(jnp.float32)
        t = jnp.tanh(math.sqrt(2 / math.pi) * (c + 0.044715 * (c * c * c)))
        hg[b, cx, mine] = (0.5 * c * (1.0 + t)).astype(jnp.bfloat16)
        t_hy(b, mine).start()
        t_hx(b, cx, mine).start()

    def pass_on_y(n):
        b = block(n, cx)
        t_hy(b, other).wait_recv()
        t_gx(b, cx, other).start()
        t_d0(b, cx).start()

    def pass_on_x(n):
        b = block(n, xp)
        t_hx(b, xp, mine).wait_recv()
        t_gx(b, xp, other).wait_recv()
        t_d1(b, xp).start()

    def second_matmul(b):
        t_d0(b, sib).wait_recv()
        t_d1(b, sibxp).wait_recv()
        acc = jnp.dot(hg[b, 0], w2[pl.ds(0, width)], preferred_element_type=jnp.float32)
        for c in range(1, 4):
            acc += jnp.dot(hg[b, c], w2[pl.ds(c * width, width)], preferred_element_type=jnp.float32)
        zp[b] = acc

    def z_send(b):
        @when(b // 4 > z)
        def _():
            t_zu(b).start()

        @when(b // 4 < z)
        def _():
            t_zn(b).start()

    def z_add(b):
        @when(b // 4 > z)
        def _():
            t_zu(b).wait_recv()
            zp[b] += zu[b]

        @when(b // 4 < z)
        def _():
            t_zn(b).wait_recv()
            zp[b] += zd[b]

        z_send(b)

    def finish(q):
        b = z * 4 + q

        @when(z > 0)
        def _():
            t_zu(b).wait_recv()
            zp[b] += zu[b]

        @when(z < 3)
        def _():
            t_zn(b).wait_recv()
            zp[b] += zd[b]

        @when(q == cx)
        def _():
            ab[q] = zp[b].astype(jnp.bfloat16)

        @when(q != cx)
        def _():
            fb[q] = zp[b].astype(jnp.bfloat16)
            rc(fb.at[q], ab.at[cx], a_s.at[q], a_r.at[cx], (z, y, q)).start()

    loads[1].wait()
    loads[2].wait()

    def step(i, carry):
        t = i - LEAD

        @when((t >= 0) & (t < BLOCKS))
        def _():
            activation(t)

        @when((t >= 1) & (t < BLOCKS + 1))
        def _():
            pass_on_y(t - 1)

        @when((t >= 2) & (t < BLOCKS + 2))
        def _():
            pass_on_x(t - 2)

        @when(t == 0)
        def _():
            x_from_partner()
            x_hop(1, cx)

        @when(t == 2)
        def _():
            x_hop(1, xp)
            x_hop(2, cx)

        @when(t == 4)
        def _():
            x_hop(2, xp)

        @when(t == 6)
        def _():
            x_hop(3, cx)
            x_hop(3, xp)

        @when(t == 7)
        def _():
            x_late()

        @when(t + LEAD < BLOCKS)
        def _():
            first_matmul(t + LEAD)

        n = t - 3
        group = (n == 3) | (n == 7)
        begin = jnp.where(group, n - 3, n)
        end = jnp.where((n > 7) | group, n + 1, begin)
        end = jnp.where(n < BLOCKS, end, begin)

        def one(m, carry):
            b = block(m, cx)
            second_matmul(b)

            @when(edge & (m > 3))
            def _():
                z_send(b)

            return carry

        lax.fori_loop(begin, end, one, 0)

        inner = jnp.logical_not(edge)

        @when(inner & (t >= 12) & (t < 16))
        def _():
            z_add(block(t - 8, cx))
            z_add(block(t - 4, cx))

        @when(inner & (n >= 12) & (n < 16))
        def _():
            z_add(block(n, cx))

        @when(t >= 16)
        def _():
            finish(t - 16)

        return carry

    lax.fori_loop(0, BLOCKS + 4 + LEAD, step, 0)

    def collect(c, carry):
        @when(c != cx)
        def _():
            rc(fb.at[c], ab.at[c], a_s.at[c], a_r.at[c], (z, y, c)).wait()

        return carry

    lax.fori_loop(0, 4, collect, 0)
    for c in range(4):
        out_ref[:, c * ab.shape[2]:(c + 1) * ab.shape[2]] = ab[c]

    def drain(b, carry):
        t_c(b).wait_send()
        t_hy(b, mine).wait_send()
        t_hx(b, cx, mine).wait_send()
        t_gx(b, cx, other).wait_send()
        t_d0(b, cx).wait_send()
        t_d1(b, xp).wait_send()
        p = b // 4

        @when(p != z)
        def _():
            t_zu(b).wait_send()

        @when((b + cx) % 2 == 0)
        def _():
            t_xd(b).wait_send()

            @when((z < 3) & (p <= z))
            def _():
                t_xu(b).wait_send()

            @when((z > 0) & (p >= z))
            def _():
                t_xn(b).wait_send()

        return carry

    lax.fori_loop(0, BLOCKS, drain, 0)
    t_xx(own).wait_send()


def solution(mesh):
    def body(x, w1, w2):
        dma = pltpu.SemaphoreType.DMA
        bf, f32 = jnp.bfloat16, jnp.float32
        depth, width = w1.shape
        cols = w2.shape[1]
        return pl.pallas_call(
            kernel,
            out_shape=jax.ShapeDtypeStruct(x.shape, bf),
            in_specs=[pl.BlockSpec(memory_space=pl.ANY)] * 3,
            out_specs=pl.BlockSpec(memory_space=pltpu.VMEM),
            scratch_shapes=[
                pltpu.VMEM((BLOCKS, ROWS, depth), bf),
                pltpu.VMEM(w1.shape, bf),
                pltpu.VMEM(w2.shape, bf),
                pltpu.VMEM((BLOCKS, ROWS, width), f32),
                pltpu.VMEM((BLOCKS, HALF, width), f32),
                pltpu.VMEM((BLOCKS, 4, ROWS, width), bf),
                pltpu.VMEM((BLOCKS, ROWS, cols), f32),
                pltpu.VMEM((BLOCKS, ROWS, cols), f32),
                pltpu.VMEM((BLOCKS, ROWS, cols), f32),
                pltpu.VMEM((4, ROWS, cols), bf),
                pltpu.VMEM((4, ROWS, cols), bf),
                dma((3,)), dma, dma,
            ] + [dma((BLOCKS,))] * 21 + [dma((4,)), dma((4,))],
            compiler_params=pltpu.CompilerParams(
                collective_id=0, has_side_effects=True, vmem_limit_bytes=56 * 2**20),
        )(x, w1, w2)

    return jax.shard_map(
        body,
        mesh=mesh,
        in_specs=(P(("cx", "cz"), "cy"), P("cy", ("cz", "cx")), P("cz", ("cy", "cx"))),
        out_specs=P(("cx", "cz"), "cy"),
        check_vma=False,
    )
```

time: 422 us -> 133 us (0.32)
  waiting for transfers between devices: 379 us -> 0 us
  Pallas kernels: 0 us -> 132 us
  matrix products: 24.8 us -> 0 us
  between operations: 13.5 us -> 0.01 us
  other arithmetic: 4.98 us -> 0 us
    all_gather x4 -> x0, waiting for transfers between devices: 279 us -> none  [the longest x1 108 us: body(): w1g = lax.all_gather(w1, 'cx', axis=1, tiled=True)]
    pallas_call x0 -> x1, Pallas kernels: none -> 132 us  [body(): pl.pallas_call(kernel, out_shape=jax.ShapeDtypeStruct(x.shape, bf), in_sp...]
    reduce_scatter x2 -> x0, waiting for transfers between devices: 97.9 us -> none  [the longest x1 53.8 us: body(): lax.psum_scatter(cp, 'cy', scatter_dimension=0, tiled=True)]
    dot_general x2 -> x0, matrix products: 24.8 us -> none  [the longest x1 12.5 us: body(): cp = jnp.dot(xg, w1g, preferred_element_type=jnp.float32)]
    convert_element_type x2 -> x0, other arithmetic: 4.98 us -> none  [the longest x1 3.21 us: body(): jax.nn.gelu(c.astype(jnp.float32), approximate=True).astype(jnp.bfloat16)]
  transfers between devices with their start and end apart: 6 -> 0, of which waited for: 6 -> 0; matrix products, arithmetic and copies ran while one was open for 1% -> 0% of each run, Pallas kernels for 0% -> 0%
where the time goes in v1:
time: 133 us
  Pallas kernels  132 us (99%)
  local copies, waits for them, and re-layouts  1.67 us (1%)
    pallas_call x1, Pallas kernels, body(): pl.pallas_call(kernel, out_shape=jax.ShapeDtypeStruct(x.shape, bf), in_sp...  132 us

profile of v1, /device:TPU:0, one launch (start us, length us, event | category | flops | bytes accessed | tf_op | source)
XLA Modules:
  0.0 133.4 jit_solution(14465958019699671548)
XLA Ops:
  0.0 131.7 %shard_map.37 = bf16[64,2048]{1,0:T(8,128)(2,1)} custom-call(bf16[64,2048]{1,0:T(8,128)(2,1)} %x_hbm.1, bf16[2048,1024]{1,0:T(8,128)(2,1)} %w1_hbm.1, bf16[4096,512]{1,0:T(8,128)(2,1)} %w2_hbm.1), custom_call_target="tpu_custom_call" | custom-call | tf_op jit(solution)/shard_map/pallas_call | solution.py:387
  131.7 1.7 %copy.5 = bf16[64,2048]{1,0:T(8,128)(2,1)} copy(bf16[64,2048]{1,0:T(8,128)(2,1)} %shard_map.37) | data formatting | bytes 524288

commit v2 on v1

v2 whole, which is shorter than its diff:
```python
import math

import jax
import jax.numpy as jnp
from jax import lax
from jax.experimental import pallas as pl
from jax.experimental.pallas import tpu as pltpu
from jax.sharding import PartitionSpec as P

MESH = pl.DeviceIdType.MESH
ROWS = 64
HALF = ROWS // 2
BLOCKS = 16


def kernel(x_hbm, w1_hbm, w2_hbm, out_ref, xg, w1, w2, cp, crv, hg, zp, zu, zd, fb, ab, ld,
           sent, xr, cr, hyr, hxr, dr, zr, ar):
    z, y, cx = lax.axis_index("cz"), lax.axis_index("cy"), lax.axis_index("cx")
    core = cx % 2
    xp = (cx + 2) % 4
    sib = cx + 1 - 2 * core
    sibxp = (sib + 2) % 4
    dev_y = (z, 1 - y, cx)
    dev_x = (z, y, xp)
    dev_s = (z, y, sib)
    dev_up = ((z + 1) % 4, y, cx)
    dev_dn = ((z + 3) % 4, y, cx)
    width = w1.shape[1]
    slot, slot_xp = core * 2 + cx // 2, core * 2 + 1 - cx // 2
    pair_sib = pl.ds((1 - core) * 2, 2)

    loads = [pltpu.make_async_copy(x_hbm, xg.at[z * 4 + cx], ld.at[0]),
             pltpu.make_async_copy(w1_hbm, w1, ld.at[1]),
             pltpu.make_async_copy(w2_hbm, w2, ld.at[2])]
    for load in loads:
        load.start()

    barrier = pltpu.get_barrier_semaphore()
    for dev in (dev_y, dev_x, dev_s, (z, y, sibxp)):
        pl.semaphore_signal(barrier, inc=1, device_id=dev, device_id_type=MESH)

    @pl.when(z < 3)
    def _():
        pl.semaphore_signal(barrier, inc=1, device_id=dev_up, device_id_type=MESH)

    @pl.when(z > 0)
    def _():
        pl.semaphore_signal(barrier, inc=1, device_id=dev_dn, device_id_type=MESH)

    edge = (z == 0) | (z == 3)

    inner = jnp.logical_not(edge)

    @pl.when(edge)
    def _():
        pl.semaphore_wait(barrier, 5)

    @pl.when(inner)
    def _():
        pl.semaphore_wait(barrier, 6)

    def rc(src, dst, ssem, rsem, dev):
        return pltpu.make_async_remote_copy(src_ref=src, dst_ref=dst, send_sem=ssem, recv_sem=rsem,
                                            device_id=dev, device_id_type=MESH)

    mine = pl.ds(pl.multiple_of(y * HALF, HALF), HALF)
    other = pl.ds(pl.multiple_of((1 - y) * HALF, HALF), HALF)

    def t_xx(b):
        return rc(xg.at[b], xg.at[b], sent.at[0], xr.at[b], dev_x)

    def t_xd(b):
        return rc(xg.at[b], xg.at[b], sent.at[1], xr.at[b], dev_s)

    def t_xu(b):
        return rc(xg.at[b], xg.at[b], sent.at[2], xr.at[b], dev_up)

    def t_xn(b):
        return rc(xg.at[b], xg.at[b], sent.at[3], xr.at[b], dev_dn)

    def t_c(b):
        return rc(cp.at[b, other], crv.at[b], sent.at[4], cr.at[b], dev_y)

    def t_hy(b, rows):
        return rc(hg.at[b, slot, rows], hg.at[b, slot, rows], sent.at[5], hyr.at[b], dev_y)

    def t_hx(b, rows):
        return rc(hg.at[b, slot, rows], hg.at[b, slot, rows], sent.at[6], hxr.at[b], dev_x)

    def t_hd(b, c):
        return rc(hg.at[b, c], hg.at[b, c], sent.at[7], dr.at[b], dev_s)

    def t_zu(b):
        return rc(zp.at[b], zu.at[b], sent.at[8], zr.at[b], dev_up)

    def t_zn(b, last):
        return rc(zp.at[b], zd.at[b], sent.at[8], zr.at[jnp.where(last, BLOCKS + b % 4, b)], dev_dn)

    def t_a(q, frm):
        return rc(fb.at[q], ab.at[frm], sent.at[9], ar.at[frm], (z, y, q))

    low = 1 - z // 2

    def plane(s):
        return jnp.where(s == 0, z, jnp.where(s == 1, 1 + low, jnp.where(s == 2, 3 * low, z + 1 - 2 * (z % 2))))

    def xor(a, b):
        return ((a // 2 + b // 2) % 2) * 2 + (a + b) % 2

    def block(n, me):
        s, j = n // 4, n % 4
        return plane(s) * 4 + jnp.where(s < 2, xor(me, j), j)

    def when(cond):
        return pl.when(cond)

    loads[0].wait()
    own = z * 4 + cx
    far = z * 4 + xp
    t_xx(own).start()
    t_xd(own).start()

    @when(z < 3)
    def _():
        t_xu(own).start()

    @when(z > 0)
    def _():
        t_xn(own).start()

    def x_from_partner():
        t_xx(far).wait_recv()
        t_xd(far).start()

        @when(z < 2)
        def _():
            t_xu(far).start()

        @when(z > 1)
        def _():
            t_xn(far).start()

    def x_late():
        @when(z == 2)
        def _():
            t_xu(far).start()

        @when(z == 1)
        def _():
            t_xn(far).start()

    def x_hop(dist, c, where=True):
        @when((z >= dist) & where)
        def _():
            b = (z - dist) * 4 + c
            t_xu(b).wait_recv()
            t_xd(b).start()

            @when(z < 3)
            def _():
                t_xu(b).start()

        @when((z + dist < 4) & where)
        def _():
            b = (z + dist) * 4 + c
            t_xn(b).wait_recv()
            t_xd(b).start()

            @when(z > 0)
            def _():
                t_xn(b).start()

    def first_matmul(n):
        b = block(n, cx)

        @when((b + cx) % 2 == 1)
        def _():
            t_xd(b).wait_recv()

        cp[b] = jnp.dot(xg[b], w1[...], preferred_element_type=jnp.float32)
        t_c(b).start()

    def activation(n):
        b = block(n, cx)
        t_c(b).wait_recv()
        c = (cp[b, mine] + crv[b]).astype(jnp.bfloat16).astype(jnp.float32)
        t = jnp.tanh(math.sqrt(2 / math.pi) * (c + 0.044715 * (c * c * c)))
        hg[b, slot, mine] = (0.5 * c * (1.0 + t)).astype(jnp.bfloat16)
        t_hy(b, mine).start()
        t_hx(b, mine).start()

    def pass_on_y(n):
        b = block(n, cx)
        t_hy(b, other).wait_recv()
        t_hx(b, other).start()
        t_hd(b, slot).start()

    def pass_on_x(n):
        b = block(n, xp)
        piece = hg.at[b, slot_xp]
        rc(piece, piece, sent.at[6], hxr.at[b], dev_x).wait_recv()
        t_hd(b, slot_xp).start()

    def second_matmul(b):
        pieces = hg.at[b, pair_sib]
        rc(pieces, pieces, sent.at[7], dr.at[b], dev_s).wait_recv()
        acc = jnp.dot(hg[b, 0], w2[pl.ds(0, width)], preferred_element_type=jnp.float32)
        for i in range(1, 4):
            c = (i % 2) * 2 + i // 2
            acc += jnp.dot(hg[b, i], w2[pl.ds(c * width, width)], preferred_element_type=jnp.float32)
        zp[b] = acc

    def z_send(b):
        @when(b // 4 > z)
        def _():
            t_zu(b).start()

        @when(b // 4 < z)
        def _():
            t_zn(b, b // 4 == z - 1).start()

    def z_add(b):
        @when(b // 4 > z)
        def _():
            t_zu(b).wait_recv()
            zp[b] += zu[b]

        @when(b // 4 < z)
        def _():
            t_zn(b, False).wait_recv()
            zp[b] += zd[b]

        z_send(b)

    def finish(q):
        b = z * 4 + q

        @when(z > 0)
        def _():
            t_zu(b).wait_recv()
            zp[b] += zu[b]

        @when(z < 3)
        def _():
            t_zn(b, True).wait_recv()
            zp[b] += zd[b]

        @when(q == cx)
        def _():
            ab[q] = zp[b].astype(jnp.bfloat16)

        @when(q != cx)
        def _():
            fb[q] = zp[b].astype(jnp.bfloat16)
            t_a(q, cx).start()

    loads[1].wait()

    def lead(t):
        return jnp.minimum(BLOCKS, t + 2 + jnp.clip(t - 12, 0, 1))

    def partial_c(n, carry):
        first_matmul(n)
        return carry

    def partial_z(b):
        second_matmul(b)

        @when(edge & (b // 4 != z))
        def _():
            z_send(b)

    away = plane(1) * 4

    def step(i, carry):
        t = i - 2

        @when((t >= 0) & (t < BLOCKS))
        def _():
            activation(t)

        @when(t == 0)
        def _():
            x_from_partner()
            x_hop(1, cx)

        @when(t == 2)
        def _():
            x_hop(1, xp, inner)
            x_hop(2, cx, edge)

        @when(t == 3)
        def _():
            x_hop(2, cx, inner)

        @when(t == 4)
        def _():
            x_hop(2, xp)

        @when(t == 6)
        def _():
            x_hop(3, cx)
            x_hop(3, xp)

        @when(t == 7)
        def _():
            x_late()

        @when(t == 9)
        def _():
            x_hop(1, xp, edge)

        lax.fori_loop(jnp.where(t == -2, 0, lead(t)), lead(t + 1), partial_c, 0)

        @when(t == 5)
        def _():
            loads[2].wait()

        one = (t >= 6) & (t < 19)
        two = (t == 10) | (t == 12) | (t == 14)

        def partial(m, carry):
            own_b = z * 4 + t - 6
            far_b = away + jnp.where(t == 10, m, t // 2 - 4)
            late_b = block(t - 3, cx)
            partial_z(jnp.where(t < 10, own_b, jnp.where((t == 10) | (m == 1), far_b, late_b)))
            return carry

        lax.fori_loop(0, jnp.where(two, 2, jnp.where(one, 1, 0)), partial, 0)

        @when(inner & (t >= 15) & (t < 19))
        def _():
            z_add(block(t - 3, cx))

        @when((t >= 1) & (t < BLOCKS + 1))
        def _():
            pass_on_y(t - 1)

        @when((t >= 2) & (t < BLOCKS + 2))
        def _():
            pass_on_x(t - 2)

        @when(inner & (t == 12))
        def _():
            z_add(away)
            z_add(away + 1)

        @when(inner & ((t == 14) | (t == 16)))
        def _():
            z_add(away + t // 2 - 5)

        @when(inner & ((t == 13) | (t == 14)))
        def _():
            z_add(block(t - 5, cx))

        @when(inner & ((t == 14) | (t == 15)))
        def _():
            z_add(block(t - 4, cx))

        @when(t >= 18)
        def _():
            finish(t - 18)

        return carry

    lax.fori_loop(0, BLOCKS + 8, step, 0)

    def collect(c, carry):
        @when(c != cx)
        def _():
            t_a(c, c).wait_recv()

        return carry

    lax.fori_loop(0, 4, collect, 0)
    def gather_out():
        for c in range(4):
            out_ref[:, c * ab.shape[2]:(c + 1) * ab.shape[2]] = ab[c]

    gather_out()

    def sent_all(kind, ref, dev):
        rc(ref, ref, sent.at[kind], xr.at[0], dev).wait_send()

    def wait_sends():
        sent_all(0, xg.at[own], dev_x)
        sent_all(1, xg.at[pl.ds(0, 8)], dev_s)
        for k in range(4):
            @when(z == k)
            def _(k=k):
                if k < 3:
                    sent_all(2, xg.at[pl.ds(0, 2 * (k + 1))], dev_up)
                if k > 0:
                    sent_all(3, xg.at[pl.ds(0, 2 * (4 - k))], dev_dn)
        sent_all(4, crv, dev_y)
        sent_all(5, hg.at[pl.ds(0, 2)], dev_y)
        sent_all(6, hg.at[pl.ds(0, 4)], dev_x)
        sent_all(7, hg.at[pl.ds(0, 8)], dev_s)
        sent_all(8, zp.at[pl.ds(0, 12)], dev_y)
        sent_all(9, fb.at[pl.ds(0, 3)], dev_x)

    wait_sends()


def solution(mesh):
    def body(x, w1, w2):
        dma = pltpu.SemaphoreType.DMA
        bf, f32 = jnp.bfloat16, jnp.float32
        depth, width = w1.shape
        cols = w2.shape[1]
        return pl.pallas_call(
            kernel,
            out_shape=jax.ShapeDtypeStruct(x.shape, bf),
            in_specs=[pl.BlockSpec(memory_space=pltpu.HBM)] * 3,
            out_specs=pl.BlockSpec(memory_space=pltpu.VMEM),
            scratch_shapes=[
                pltpu.VMEM((BLOCKS, ROWS, depth), bf),
                pltpu.VMEM(w1.shape, bf),
                pltpu.VMEM(w2.shape, bf),
                pltpu.VMEM((BLOCKS, ROWS, width), f32),
                pltpu.VMEM((BLOCKS, HALF, width), f32),
                pltpu.VMEM((BLOCKS, 4, ROWS, width), bf),
                pltpu.VMEM((BLOCKS, ROWS, cols), f32),
                pltpu.VMEM((BLOCKS, ROWS, cols), f32),
                pltpu.VMEM((BLOCKS, ROWS, cols), f32),
                pltpu.VMEM((4, ROWS, cols), bf),
                pltpu.VMEM((4, ROWS, cols), bf),
                dma((3,)), dma((10,)),
            ] + [dma((BLOCKS,))] * 5 + [dma((BLOCKS + 4,)), dma((4,))],
            compiler_params=pltpu.CompilerParams(
                collective_id=0, has_side_effects=True, vmem_limit_bytes=56_150_000),
        )(x, w1, w2)

    return jax.shard_map(
        body,
        mesh=mesh,
        in_specs=(P(("cx", "cz"), "cy"), P("cy", ("cz", "cx")), P("cz", ("cy", "cx"))),
        out_specs=P(("cx", "cz"), "cy"),
        check_vma=False,
    )
```

time: 133 us -> 95.3 us (0.72)
  Pallas kernels: 132 us -> 94.4 us
    pallas_call x1, Pallas kernels: 132 us -> 94.4 us  [body(): pl.pallas_call(kernel, out_shape=jax.ShapeDtypeStruct(x.shape, bf), in_sp...]
where the time goes in v2:
time: 95.3 us; the launch traced here: 95.1 us
  Pallas kernels  94.4 us (99%)
    pallas_call x1, Pallas kernels, body(): pl.pallas_call(kernel, out_shape=jax.ShapeDtypeStruct(x.shape, bf), in_sp...  94.4 us

profile of v2, /device:TPU:0, one launch (start us, length us, event | category | flops | bytes accessed | tf_op | source)
XLA Modules:
  0.0 95.1 jit_solution(14807683280281901903)
XLA Ops:
  0.0 94.4 %shard_map.37 = bf16[64,2048]{1,0:T(8,128)(2,1)S(1)} custom-call(bf16[64,2048]{1,0:T(8,128)(2,1)} %x_hbm.1, bf16[2048,1024]{1,0:T(8,128)(2,1)} %w1_hbm.1, bf16[4096,512]{1,0:T(8,128)(2,1)} %w2_hbm.1), custom_call_target="tpu_custom_call" | custom-call | tf_op jit(solution)/shard_map/pallas_call | solution.py:411
  94.4 0.7 copy.5

commit v3 on v2

--- a/solution.py
+++ b/solution.py
@@ -19,24 +19,26 @@
     core = cx % 2
     xp = (cx + 2) % 4
     sib = cx + 1 - 2 * core
-    sibxp = (sib + 2) % 4
     dev_y = (z, 1 - y, cx)
     dev_x = (z, y, xp)
     dev_s = (z, y, sib)
     dev_up = ((z + 1) % 4, y, cx)
     dev_dn = ((z + 3) % 4, y, cx)
     width = w1.shape[1]
+    left, right = pl.ds(0, width // 2), pl.ds(width // 2, width // 2)
     slot, slot_xp = core * 2 + cx // 2, core * 2 + 1 - cx // 2
     pair_sib = pl.ds((1 - core) * 2, 2)
 
     loads = [pltpu.make_async_copy(x_hbm, xg.at[z * 4 + cx], ld.at[0]),
-             pltpu.make_async_copy(w1_hbm, w1, ld.at[1]),
-             pltpu.make_async_copy(w2_hbm, w2, ld.at[2])]
+             pltpu.make_async_copy(w1_hbm.at[:, left], w1.at[:, left], ld.at[1]),
+             pltpu.make_async_copy(w1_hbm.at[:, right], w1.at[:, right], ld.at[2]),
+             pltpu.make_async_copy(w2_hbm, w2, ld.at[3])]
     for load in loads:
         load.start()
 
     barrier = pltpu.get_barrier_semaphore()
-    for dev in (dev_y, dev_x, dev_s, (z, y, sibxp)):
+    near = z + 1 - 2 * (z % 2)
+    for dev in (dev_y, dev_x, dev_s, (near, y, xp), (near, y, sib), (near, y, (sib + 2) % 4)):
         pl.semaphore_signal(barrier, inc=1, device_id=dev, device_id_type=MESH)
 
     @pl.when(z < 3)
@@ -53,11 +55,11 @@
 
     @pl.when(edge)
     def _():
-        pl.semaphore_wait(barrier, 5)
+        pl.semaphore_wait(barrier, 7)
 
     @pl.when(inner)
     def _():
-        pl.semaphore_wait(barrier, 6)
+        pl.semaphore_wait(barrier, 8)
 
     def rc(src, dst, ssem, rsem, dev):
         return pltpu.make_async_remote_copy(src_ref=src, dst_ref=dst, send_sem=ssem, recv_sem=rsem,
@@ -97,19 +99,19 @@
         return rc(zp.at[b], zd.at[b], sent.at[8], zr.at[jnp.where(last, BLOCKS + b % 4, b)], dev_dn)
 
     def t_a(q, frm):
-        return rc(fb.at[q], ab.at[frm], sent.at[9], ar.at[frm], (z, y, q))
+        return rc(fb.at[q], ab.at[frm], sent.at[9], ar.at[frm], (near, y, q))
 
     low = 1 - z // 2
 
     def plane(s):
-        return jnp.where(s == 0, z, jnp.where(s == 1, 1 + low, jnp.where(s == 2, 3 * low, z + 1 - 2 * (z % 2))))
+        return jnp.where(s == 0, z, jnp.where(s == 1, 1 + low, jnp.where(s == 2, 3 * low, near)))
 
     def xor(a, b):
         return ((a // 2 + b // 2) % 2) * 2 + (a + b) % 2
 
     def block(n, me):
         s, j = n // 4, n % 4
-        return plane(s) * 4 + jnp.where(s < 2, xor(me, j), j)
+        return plane(s) * 4 + jnp.where(s == 0, xor(me, j), jnp.where(s == 1, (me // 2 * 2 + j) % 4, j))
 
     def when(cond):
         return pl.when(cond)
@@ -210,22 +212,26 @@
             acc += jnp.dot(hg[b, i], w2[pl.ds(c * width, width)], preferred_element_type=jnp.float32)
         zp[b] = acc
 
+    def last_plane(b):
+        p = b // 4
+        return p + 1 - 2 * (p % 2)
+
     def z_send(b):
-        @when(b // 4 > z)
+        @when(last_plane(b) > z)
         def _():
             t_zu(b).start()
 
-        @when(b // 4 < z)
-        def _():
-            t_zn(b, b // 4 == z - 1).start()
+        @when(last_plane(b) < z)
+        def _():
+            t_zn(b, last_plane(b) == z - 1).start()
 
     def z_add(b):
-        @when(b // 4 > z)
+        @when(last_plane(b) > z)
         def _():
             t_zu(b).wait_recv()
             zp[b] += zu[b]
 
-        @when(b // 4 < z)
+        @when(last_plane(b) < z)
         def _():
             t_zn(b, False).wait_recv()
             zp[b] += zd[b]
@@ -233,7 +239,7 @@
         z_send(b)
 
     def finish(q):
-        b = z * 4 + q
+        b = near * 4 + q
 
         @when(z > 0)
         def _():
@@ -245,19 +251,16 @@
             t_zn(b, True).wait_recv()
             zp[b] += zd[b]
 
-        @when(q == cx)
-        def _():
-            ab[q] = zp[b].astype(jnp.bfloat16)
-
-        @when(q != cx)
-        def _():
-            fb[q] = zp[b].astype(jnp.bfloat16)
-            t_a(q, cx).start()
-
-    loads[1].wait()
+        fb[q] = zp[b].astype(jnp.bfloat16)
+        t_a(q, cx).start()
+
+    for load, cols in ((loads[1], left), (loads[2], right)):
+        load.wait()
+        cp[own, :, cols] = jnp.dot(xg[own], w1[:, cols], preferred_element_type=jnp.float32)
+        rc(cp.at[own, other, cols], crv.at[own, :, cols], sent.at[4], cr.at[own], dev_y).start()
 
     def lead(t):
-        return jnp.minimum(BLOCKS, t + 2 + jnp.clip(t - 12, 0, 1))
+        return jnp.minimum(BLOCKS, t + 2 + jnp.clip(t - 11, 0, 1))
 
     def partial_c(n, carry):
         first_matmul(n)
@@ -266,18 +269,38 @@
     def partial_z(b):
         second_matmul(b)
 
-        @when(edge & (b // 4 != z))
+        @when(edge & (b // 4 != near))
         def _():
             z_send(b)
 
     away = plane(1) * 4
 
     def step(i, carry):
-        t = i - 2
+        t = i - 1
+
+        @when(inner & (t == 11))
+        def _():
+            z_add(away)
+
+        @when(t == 15)
+        def _():
+            pass_on_y(12)
 
         @when((t >= 0) & (t < BLOCKS))
         def _():
             activation(t)
+
+        @when(t == 16)
+        def _():
+            pass_on_y(15)
+
+        @when(inner & (t == 16))
+        def _():
+            z_add(block(11, cx))
+
+        @when(t == 17)
+        def _():
+            pass_on_x(15)
 
         @when(t == 0)
         def _():
@@ -310,66 +333,76 @@
         def _():
             x_hop(1, xp, edge)
 
-        lax.fori_loop(jnp.where(t == -2, 0, lead(t)), lead(t + 1), partial_c, 0)
+        lax.fori_loop(lead(t), lead(t + 1), partial_c, 0)
 
         @when(t == 5)
         def _():
-            loads[2].wait()
-
-        one = (t >= 6) & (t < 19)
-        two = (t == 10) | (t == 12) | (t == 14)
+            loads[3].wait()
 
         def partial(m, carry):
-            own_b = z * 4 + t - 6
-            far_b = away + jnp.where(t == 10, m, t // 2 - 4)
-            late_b = block(t - 3, cx)
-            partial_z(jnp.where(t < 10, own_b, jnp.where((t == 10) | (m == 1), far_b, late_b)))
+            own_b = z * 4 + jnp.where(t == 6, m, t - 5)
+            late = block(t - 3 - t // 16 + t // 17, cx)
+            partial_z(jnp.where(t < 9, own_b, jnp.where(t < 11, away + t - 9 + 2 * m, late)))
             return carry
 
-        lax.fori_loop(0, jnp.where(two, 2, jnp.where(one, 1, 0)), partial, 0)
-
-        @when(inner & (t >= 15) & (t < 19))
-        def _():
-            z_add(block(t - 3, cx))
-
-        @when((t >= 1) & (t < BLOCKS + 1))
+        two = (t == 6) | (t == 9) | (t == 10)
+        lax.fori_loop(0, jnp.where(two, 2, jnp.where((t >= 6) & (t != 15), 1, 0)), partial, 0)
+
+        @when(t == 16)
+        def _():
+            finish(0)
+            pass_on_x(13)
+            pass_on_x(14)
+            partial_z(block(13, cx))
+
+        @when(inner & (t == 12))
+        def _():
+            z_add(away + 1)
+
+        @when((t >= 1) & (t < 13))
         def _():
             pass_on_y(t - 1)
 
-        @when((t >= 2) & (t < BLOCKS + 2))
+        @when((t >= 2) & (t < 14))
         def _():
             pass_on_x(t - 2)
 
-        @when(inner & (t == 12))
-        def _():
-            z_add(away)
-            z_add(away + 1)
-
-        @when(inner & ((t == 14) | (t == 16)))
-        def _():
-            z_add(away + t // 2 - 5)
-
-        @when(inner & ((t == 13) | (t == 14)))
+        @when(t == 15)
+        def _():
+            pass_on_y(13)
+            pass_on_y(14)
+
+        @when(inner & ((t == 11) | (t == 12)))
+        def _():
+            z_add(away + t - 9)
+
+        @when(inner & (t >= 13) & (t < 16))
         def _():
             z_add(block(t - 5, cx))
 
+        @when(inner & (t == 13))
+        def _():
+            z_add(z * 4)
+            z_add(z * 4 + 2)
+
         @when(inner & ((t == 14) | (t == 15)))
         def _():
-            z_add(block(t - 4, cx))
-
-        @when(t >= 18)
-        def _():
-            finish(t - 18)
+            z_add(z * 4 + 2 * t - 27)
+
+        @when(t == 15)
+        def _():
+            pass_on_x(12)
+
+        @when(t >= 16)
+        def _():
+            finish(t - 15)
 
         return carry
 
-    lax.fori_loop(0, BLOCKS + 8, step, 0)
+    lax.fori_loop(0, BLOCKS + 4, step, 0)
 
     def collect(c, carry):
-        @when(c != cx)
-        def _():
-            t_a(c, c).wait_recv()
-
+        t_a(c, c).wait_recv()
         return carry
 
     lax.fori_loop(0, 4, collect, 0)
@@ -397,7 +430,7 @@
         sent_all(6, hg.at[pl.ds(0, 4)], dev_x)
         sent_all(7, hg.at[pl.ds(0, 8)], dev_s)
         sent_all(8, zp.at[pl.ds(0, 12)], dev_y)
-        sent_all(9, fb.at[pl.ds(0, 3)], dev_x)
+        sent_all(9, fb, dev_x)
 
     wait_sends()
 
@@ -425,7 +458,7 @@
                 pltpu.VMEM((BLOCKS, ROWS, cols), f32),
                 pltpu.VMEM((4, ROWS, cols), bf),
                 pltpu.VMEM((4, ROWS, cols), bf),
-                dma((3,)), dma((10,)),
+                dma((4,)), dma((10,)),
             ] + [dma((BLOCKS,))] * 5 + [dma((BLOCKS + 4,)), dma((4,))],
             compiler_params=pltpu.CompilerParams(
                 collective_id=0, has_side_effects=True, vmem_limit_bytes=56_150_000),

time: 95.3 us -> 87.6 us (0.919)
  Pallas kernels: 94.4 us -> 86.6 us
    pallas_call x1, Pallas kernels: 94.4 us -> 86.6 us  [body(): pl.pallas_call(kernel, out_shape=jax.ShapeDtypeStruct(x.shape, bf), in_sp...]
where the time goes in v3:
time: 87.6 us; the launch traced here: 87.3 us
  Pallas kernels  86.6 us (99%)
    pallas_call x1, Pallas kernels, body(): pl.pallas_call(kernel, out_shape=jax.ShapeDtypeStruct(x.shape, bf), in_sp...  86.6 us

profile of v3, /device:TPU:0, one launch (start us, length us, event | category | flops | bytes accessed | tf_op | source)
XLA Modules:
  0.0 87.3 jit_solution(6834922919172684857)
XLA Ops:
  0.0 86.6 %shard_map.37 = bf16[64,2048]{1,0:T(8,128)(2,1)S(1)} custom-call(bf16[64,2048]{1,0:T(8,128)(2,1)} %x_hbm.1, bf16[2048,1024]{1,0:T(8,128)(2,1)} %w1_hbm.1, bf16[4096,512]{1,0:T(8,128)(2,1)} %w2_hbm.1), custom_call_target="tpu_custom_call" | custom-call | tf_op jit(solution)/shard_map/pallas_call | solution.py:444
  86.6 0.7 copy.5

commit v4 on v3

--- a/solution.py
+++ b/solution.py
@@ -31,8 +31,7 @@
 
     loads = [pltpu.make_async_copy(x_hbm, xg.at[z * 4 + cx], ld.at[0]),
              pltpu.make_async_copy(w1_hbm.at[:, left], w1.at[:, left], ld.at[1]),
-             pltpu.make_async_copy(w1_hbm.at[:, right], w1.at[:, right], ld.at[2]),
-             pltpu.make_async_copy(w2_hbm, w2, ld.at[3])]
+             pltpu.make_async_copy(w1_hbm.at[:, right], w1.at[:, right], ld.at[2])]
     for load in loads:
         load.start()
 
@@ -68,6 +67,10 @@
     mine = pl.ds(pl.multiple_of(y * HALF, HALF), HALF)
     other = pl.ds(pl.multiple_of((1 - y) * HALF, HALF), HALF)
 
+    def turn(b):
+        p = b // 4
+        return b % 4 + jnp.where((p == near) | (p == 2 - z // 2), 4, 0)
+
     def t_xx(b):
         return rc(xg.at[b], xg.at[b], sent.at[0], xr.at[b], dev_x)
 
@@ -81,16 +84,16 @@
         return rc(xg.at[b], xg.at[b], sent.at[3], xr.at[b], dev_dn)
 
     def t_c(b):
-        return rc(cp.at[b, other], crv.at[b], sent.at[4], cr.at[b], dev_y)
+        return rc(cp.at[b, other], crv.at[b], sent.at[4], cr.at[turn(b)], dev_y)
 
     def t_hy(b, rows):
-        return rc(hg.at[b, slot, rows], hg.at[b, slot, rows], sent.at[5], hyr.at[b], dev_y)
+        return rc(hg.at[b, slot, rows], hg.at[b, slot, rows], sent.at[5], hyr.at[turn(b)], dev_y)
 
     def t_hx(b, rows):
-        return rc(hg.at[b, slot, rows], hg.at[b, slot, rows], sent.at[6], hxr.at[b], dev_x)
+        return rc(hg.at[b, slot, rows], hg.at[b, slot, rows], sent.at[6], hxr.at[turn(b)], dev_x)
 
     def t_hd(b, c):
-        return rc(hg.at[b, c], hg.at[b, c], sent.at[7], dr.at[b], dev_s)
+        return rc(hg.at[b, c], hg.at[b, c], sent.at[7], dr.at[turn(b)], dev_s)
 
     def t_zu(b):
         return rc(zp.at[b], zu.at[b], sent.at[8], zr.at[b], dev_up)
@@ -106,12 +109,11 @@
     def plane(s):
         return jnp.where(s == 0, z, jnp.where(s == 1, 1 + low, jnp.where(s == 2, 3 * low, near)))
 
-    def xor(a, b):
-        return ((a // 2 + b // 2) % 2) * 2 + (a + b) % 2
-
     def block(n, me):
         s, j = n // 4, n % 4
-        return plane(s) * 4 + jnp.where(s == 0, xor(me, j), jnp.where(s == 1, (me // 2 * 2 + j) % 4, j))
+        chip = me // 2 * 2
+        own_first = chip + jnp.where(s == 1, j + 1 - 2 * (j % 2), jnp.where(j < 2, (me + j) % 2, j))
+        return plane(s) * 4 + jnp.where(s < 2, own_first % 4, j)
 
     def when(cond):
         return pl.when(cond)
@@ -119,16 +121,24 @@
     loads[0].wait()
     own = z * 4 + cx
     far = z * 4 + xp
-    t_xx(own).start()
     t_xd(own).start()
 
-    @when(z < 3)
-    def _():
-        t_xu(own).start()
-
-    @when(z > 0)
-    def _():
-        t_xn(own).start()
+    def x_line():
+        @when(z < 3)
+        def _():
+            t_xu(own).start()
+
+        @when(z > 0)
+        def _():
+            t_xn(own).start()
+
+    @when(core == 0)
+    def _():
+        t_xx(own).start()
+
+    @when(core == 1)
+    def _():
+        x_line()
 
     def x_from_partner():
         t_xx(far).wait_recv()
@@ -200,12 +210,12 @@
     def pass_on_x(n):
         b = block(n, xp)
         piece = hg.at[b, slot_xp]
-        rc(piece, piece, sent.at[6], hxr.at[b], dev_x).wait_recv()
+        rc(piece, piece, sent.at[6], hxr.at[turn(b)], dev_x).wait_recv()
         t_hd(b, slot_xp).start()
 
     def second_matmul(b):
         pieces = hg.at[b, pair_sib]
-        rc(pieces, pieces, sent.at[7], dr.at[b], dev_s).wait_recv()
+        rc(pieces, pieces, sent.at[7], dr.at[turn(b)], dev_s).wait_recv()
         acc = jnp.dot(hg[b, 0], w2[pl.ds(0, width)], preferred_element_type=jnp.float32)
         for i in range(1, 4):
             c = (i % 2) * 2 + i // 2
@@ -257,10 +267,20 @@
     for load, cols in ((loads[1], left), (loads[2], right)):
         load.wait()
         cp[own, :, cols] = jnp.dot(xg[own], w1[:, cols], preferred_element_type=jnp.float32)
-        rc(cp.at[own, other, cols], crv.at[own, :, cols], sent.at[4], cr.at[own], dev_y).start()
+        rc(cp.at[own, other, cols], crv.at[own, :, cols], sent.at[4], cr.at[turn(own)], dev_y).start()
+
+    @when(core == 0)
+    def _():
+        x_line()
+
+    @when(core == 1)
+    def _():
+        t_xx(own).start()
+
+    first_matmul(1)
 
     def lead(t):
-        return jnp.minimum(BLOCKS, t + 2 + jnp.clip(t - 11, 0, 1))
+        return jnp.minimum(BLOCKS, t + 2 + jnp.clip(t - 11, 0, 1) + jnp.where((t == 0) & (core == 0) | (t < 0), 1, 0))
 
     def partial_c(n, carry):
         first_matmul(n)
@@ -280,7 +300,7 @@
 
         @when(inner & (t == 11))
         def _():
-            z_add(away)
+            z_add(away + 1)
 
         @when(t == 15)
         def _():
@@ -294,17 +314,16 @@
         def _():
             pass_on_y(15)
 
-        @when(inner & (t == 16))
-        def _():
-            z_add(block(11, cx))
-
         @when(t == 17)
         def _():
             pass_on_x(15)
 
-        @when(t == 0)
+        @when((t < 0) & (core == 0))
         def _():
             x_from_partner()
+
+        @when((t < 0) & (core == 1) | (t == 0) & (core == 0))
+        def _():
             x_hop(1, cx)
 
         @when(t == 2)
@@ -335,14 +354,23 @@
 
         lax.fori_loop(lead(t), lead(t + 1), partial_c, 0)
 
+        @when((t == 0) & (core == 1))
+        def _():
+            x_from_partner()
+
+        @when((t >= 1) & (t < 5))
+        def _():
+            rows = pl.ds(pl.multiple_of((t - 1) * width, width), width)
+            pltpu.make_async_copy(w2_hbm.at[rows], w2.at[rows], ld.at[3]).start()
+
         @when(t == 5)
         def _():
-            loads[3].wait()
+            pltpu.make_async_copy(w2_hbm, w2, ld.at[3]).wait()
 
         def partial(m, carry):
             own_b = z * 4 + jnp.where(t == 6, m, t - 5)
             late = block(t - 3 - t // 16 + t // 17, cx)
-            partial_z(jnp.where(t < 9, own_b, jnp.where(t < 11, away + t - 9 + 2 * m, late)))
+            partial_z(jnp.where(t < 9, own_b, jnp.where(t < 11, away + 10 - t + 2 * m, late)))
             return carry
 
         two = (t == 6) | (t == 9) | (t == 10)
@@ -357,7 +385,7 @@
 
         @when(inner & (t == 12))
         def _():
-            z_add(away + 1)
+            z_add(away + 0)
 
         @when((t >= 1) & (t < 13))
         def _():
@@ -370,28 +398,34 @@
         @when(t == 15)
         def _():
             pass_on_y(13)
+            pass_on_x(12)
+
+            @when(inner)
+            def _():
+                z_add(block(10, cx))
+
             pass_on_y(14)
 
+            @when(inner)
+            def _():
+                z_add(block(11, cx))
+
         @when(inner & ((t == 11) | (t == 12)))
         def _():
-            z_add(away + t - 9)
-
-        @when(inner & (t >= 13) & (t < 16))
+            z_add(away + 14 - t)
+
+        @when(inner & ((t == 13) | (t == 14)))
         def _():
             z_add(block(t - 5, cx))
 
         @when(inner & (t == 13))
         def _():
-            z_add(z * 4)
-            z_add(z * 4 + 2)
+            z_add(z * 4 + 1)
+            z_add(z * 4 + 3)
 
         @when(inner & ((t == 14) | (t == 15)))
         def _():
-            z_add(z * 4 + 2 * t - 27)
-
-        @when(t == 15)
-        def _():
-            pass_on_x(12)
+            z_add(z * 4 + 2 * t - 28)
 
         @when(t >= 16)
         def _():
@@ -459,7 +493,7 @@
                 pltpu.VMEM((4, ROWS, cols), bf),
                 pltpu.VMEM((4, ROWS, cols), bf),
                 dma((4,)), dma((10,)),
-            ] + [dma((BLOCKS,))] * 5 + [dma((BLOCKS + 4,)), dma((4,))],
+            ] + [dma((BLOCKS,))] + [dma((8,))] * 4 + [dma((BLOCKS + 4,)), dma((4,))],
             compiler_params=pltpu.CompilerParams(
                 collective_id=0, has_side_effects=True, vmem_limit_bytes=56_150_000),
         )(x, w1, w2)

time: 87.6 us -> 87.3 us (level)
  no operation moved by 1% of the time
where the time goes in v4:
time: 87.3 us; the launch traced here: 87.1 us
  Pallas kernels  86.4 us (99%)
    pallas_call x1, Pallas kernels, body(): pl.pallas_call(kernel, out_shape=jax.ShapeDtypeStruct(x.shape, bf), in_sp...  86.4 us

profile of v4, /device:TPU:0, one launch (start us, length us, event | category | flops | bytes accessed | tf_op | source)
XLA Modules:
  0.0 87.1 jit_solution(18372074073007808674)
XLA Ops:
  0.0 86.4 %shard_map.37 = bf16[64,2048]{1,0:T(8,128)(2,1)S(1)} custom-call(bf16[64,2048]{1,0:T(8,128)(2,1)} %x_hbm.1, bf16[2048,1024]{1,0:T(8,128)(2,1)} %w1_hbm.1, bf16[4096,512]{1,0:T(8,128)(2,1)} %w2_hbm.1), custom_call_target="tpu_custom_call" | custom-call | tf_op jit(solution)/shard_map/pallas_call | solution.py:478
  86.4 0.7 copy.5

commit v5 on v4

--- a/solution.py
+++ b/solution.py
@@ -121,8 +121,6 @@
     loads[0].wait()
     own = z * 4 + cx
     far = z * 4 + xp
-    t_xd(own).start()
-
     def x_line():
         @when(z < 3)
         def _():
@@ -139,6 +137,8 @@
     @when(core == 1)
     def _():
         x_line()
+
+    t_xd(own).start()
 
     def x_from_partner():
         t_xx(far).wait_recv()

time: 87.3 us -> 87.3 us (level)
  no operation moved by 1% of the time
where the time goes in v5:
time: 87.3 us; the launch traced here: 87.1 us
  Pallas kernels  86.4 us (99%)
    pallas_call x1, Pallas kernels, body(): pl.pallas_call(kernel, out_shape=jax.ShapeDtypeStruct(x.shape, bf), in_sp...  86.4 us

profile of v5, /device:TPU:0, one launch (start us, length us, event | category | flops | bytes accessed | tf_op | source)
XLA Modules:
  0.0 87.1 jit_solution(238376368980632858)
XLA Ops:
  0.0 86.4 %shard_map.37 = bf16[64,2048]{1,0:T(8,128)(2,1)S(1)} custom-call(bf16[64,2048]{1,0:T(8,128)(2,1)} %x_hbm.1, bf16[2048,1024]{1,0:T(8,128)(2,1)} %w1_hbm.1, bf16[4096,512]{1,0:T(8,128)(2,1)} %w2_hbm.1), custom_call_target="tpu_custom_call" | custom-call | tf_op jit(solution)/shard_map/pallas_call | solution.py:478
  86.4 0.7 copy.5
